TPU v7x, 32 devices: a whole 2x2x4 slice. The times are simulated.
32 devices in a mesh: row: 2 (over y), theta: 4 (over x, core), gz: 4 (over z).
Axes of the slice: x: 2, y: 2, z: 4, core: 2. Of those that a mesh axis runs over, the one named last changes fastest.
Arguments:
- state_start: float32 [6, 8, 128, 1024], P(None, 'row', 'gz', 'theta'), may hold values from -1.2 to 1.2
- state_section: float32 [6, 8, 128, 1024], P(None, 'row', 'gz', 'theta'), may hold values from -1.5 to 4, as said below
- phase: int32 [8, 128, 1024], P('row', 'gz', 'theta'), may hold values 0 or 1
- cutoff: int32 [4], replicated, may hold values from 1 to 63
Outputs:
- state_next: float32 [6, 8, 128, 1024], P(None, 'row', 'gz', 'theta')
Inputs may be any that keep to these rules, and one draw needn't show every extreme that they name: `state_section`: channel 0 (density) lies in 0.5 to 2.0, channels 1 to 3 (momenta) in -1.5 to 1.5, channel 4 (total energy) in 2.5 to 4.0, channel 5 (jet mass density) in 0 to 1.0.
All inputs are finite; a program needn't handle non-finite values. No bound on the sum of `phase` on one device may be relied on, other than what follows from the above.
Results may differ from a plain program's by a relative error of at most 0.0003.
Values sent between devices are 32-bit elements; how exact they have to be, the bound alone decides.
A program may use at most 64 MiB of HBM per device.

v0:
```python
import math
import jax
import jax.numpy as jnp
from jax import lax
from jax.sharding import PartitionSpec as P

NT = 1024
KMODES = 64
split_speed = 10.0
time_step = 0.05
weno_epsilon = 1e-06
liquid_ratio = 4.4
gas_ratio = 1.4
liquid_stiffness = 0.6


def passed_along(value, axis, steps):
    count = lax.axis_size(axis)
    pairs = [(source, (source + steps) % count) for source in range(count)]
    return lax.ppermute(value, axis, pairs)


def with_halo(cells, sides, width):
    for axis, dim in sides:
        count = lax.axis_size(axis)
        head = lax.slice_in_dim(cells, 0, width, axis=dim)
        tail = lax.slice_in_dim(cells, cells.shape[dim] - width, cells.shape[dim], axis=dim)
        cells = jnp.concatenate(
            [
                lax.ppermute(tail, axis, [(i, (i + 1) % count) for i in range(count)]),
                cells,
                lax.ppermute(head, axis, [((i + 1) % count, i) for i in range(count)]),
            ],
            axis=dim,
        )
    return cells


def pressure_of(state, phase):
    density = state[0]
    kinetic = 0.5 * (state[1] * state[1] + state[2] * state[2] + state[3] * state[3]) / density
    liquid = phase == 1
    heat_ratio = jnp.where(liquid, liquid_ratio, gas_ratio)
    stiffness = jnp.where(liquid, liquid_stiffness, 0.0)
    return (heat_ratio - 1.0) * (state[4] - kinetic) - heat_ratio * stiffness


def weno_face(far_left, near_left, centre, near_right, far_right):
    smooth_left = (
        13.0 / 12.0 * (far_left - 2.0 * near_left + centre) ** 2
        + 0.25 * (far_left - 4.0 * near_left + 3.0 * centre) ** 2
    )
    smooth_mid = (
        13.0 / 12.0 * (near_left - 2.0 * centre + near_right) ** 2
        + 0.25 * (near_left - near_right) ** 2
    )
    smooth_right = (
        13.0 / 12.0 * (centre - 2.0 * near_right + far_right) ** 2
        + 0.25 * (3.0 * centre - 4.0 * near_right + far_right) ** 2
    )
    weight_left = 0.1 / (weno_epsilon + smooth_left) ** 2
    weight_mid = 0.6 / (weno_epsilon + smooth_mid) ** 2
    weight_right = 0.3 / (weno_epsilon + smooth_right) ** 2
    weight_sum = weight_left + weight_mid + weight_right
    value_left = (2.0 * far_left - 7.0 * near_left + 11.0 * centre) / 6.0
    value_mid = (-near_left + 5.0 * centre + 2.0 * near_right) / 6.0
    value_right = (2.0 * centre + 5.0 * near_right - far_right) / 6.0
    return (
        weight_left * value_left + weight_mid * value_mid + weight_right * value_right
    ) / weight_sum


def face_fluxes(padded_line, array_axis, component):
    density = padded_line[0]
    velocity = padded_line[component] / density
    pressure_field = padded_line[6]
    conserved = padded_line[:6]
    flux_rows = [conserved[channel] * velocity for channel in range(6)]
    flux_rows[component] = flux_rows[component] + pressure_field
    flux_rows[4] = flux_rows[4] + pressure_field * velocity
    physical = jnp.stack(flux_rows)
    upward = 0.5 * (physical + split_speed * conserved)
    downward = 0.5 * (physical - split_speed * conserved)
    face_count = padded_line.shape[array_axis] - 5

    def shifted(values, offset):
        return lax.slice_in_dim(values, offset, offset + face_count, axis=array_axis)

    upwind_part = weno_face(
        shifted(upward, 0),
        shifted(upward, 1),
        shifted(upward, 2),
        shifted(upward, 3),
        shifted(upward, 4),
    )
    downwind_part = weno_face(
        shifted(downward, 5),
        shifted(downward, 4),
        shifted(downward, 3),
        shifted(downward, 2),
        shifted(downward, 1),
    )
    return upwind_part + downwind_part


def tendency(centre_cells, radial_line, axial_line, azimuth_line, cycle_start):
    cycle_count = centre_cells.shape[1]
    radial_flux = face_fluxes(radial_line, 1, 1)
    axial_flux = face_fluxes(axial_line, 2, 3)
    azimuth_flux = face_fluxes(azimuth_line, 3, 2)
    cycle_index = (cycle_start + lax.iota(jnp.int32, cycle_count + 1)).astype(centre_cells.dtype)
    face_radius = cycle_index[None, :, None, None]
    cell_radius = face_radius[:, :-1] + 0.5
    weighted = face_radius * radial_flux
    div_radial = (weighted[:, 1:] - weighted[:, :-1]) / cell_radius
    div_axial = axial_flux[:, :, 1:] - axial_flux[:, :, :-1]
    angle_step = 2.0 * math.pi / NT
    div_azimuth = (azimuth_flux[..., 1:] - azimuth_flux[..., :-1]) / (cell_radius * angle_step)
    density = centre_cells[0]
    swirl_speed = centre_cells[2] / density
    radius = cell_radius[0]
    source_radial = (centre_cells[2] * swirl_speed + centre_cells[6]) / radius
    source_swirl = -centre_cells[1] * swirl_speed / radius
    zero_field = jnp.zeros_like(density)
    source = jnp.stack(
        [zero_field, source_radial, source_swirl, zero_field, zero_field, zero_field]
    )
    return source - div_radial - div_axial - div_azimuth


def across_axis(partner):
    sign_flip = jnp.array([1.0, -1.0, -1.0, 1.0, 1.0, 1.0, 1.0], partner.dtype)[:, None, None, None]
    return partner[:, ::-1] * sign_flip


def build_table(positions, mode_count, length):
    orders = lax.iota(jnp.int32, mode_count)
    phases = positions[:, None] * orders[None, :] % length
    angles = phases.astype(jnp.float32) * (2.0 * math.pi / length)
    return jnp.concatenate([jnp.cos(angles), jnp.sin(angles)], 1)


def cycle_weights(cutoff, mode_count, length):
    orders = lax.iota(jnp.int32, mode_count)
    mode_scale = jnp.where(orders == 0, 1.0 / length, 2.0 / length)
    kept_modes = orders[None, :] <= cutoff[:, None]
    weight_half = jnp.where(kept_modes, mode_scale[None, :], 0.0)
    return jnp.concatenate([weight_half, weight_half], 1)


def apply_filter(cycle_block, weights, theta_id):
    local_theta = cycle_block.shape[3]
    positions = theta_id * local_theta + lax.iota(jnp.int32, local_theta)
    fourier_table = build_table(positions, KMODES, NT)
    coefficients = jnp.einsum(
        "vizt,tk->vizk", cycle_block, fourier_table, precision=lax.Precision.HIGHEST
    )
    coefficients = lax.psum(coefficients, "theta")
    coefficients = coefficients * weights[None, :, None, :]
    return jnp.einsum("vizk,tk->vizt", coefficients, fourier_table, precision=lax.Precision.HIGHEST)


def shards(state_start, state_section, phase, cutoff):
    row_count = lax.axis_size("row")
    row_id = lax.axis_index("row")
    theta_count = lax.axis_size("theta")
    theta_id = lax.axis_index("theta")
    cycle_count = state_section.shape[1]
    filtered_count = cutoff.shape[0]
    pressure_field = pressure_of(state_section, phase)
    fields = jnp.concatenate([state_section, pressure_field[None]], 0)
    partner = passed_along(fields[:, 0:3], "theta", theta_count // 2)
    mirror = across_axis(partner)
    outer_rim = jnp.repeat(fields[:, -1:], 3, axis=1)
    padded = with_halo(fields, (("row", 1), ("theta", 3), ("gz", 2)), 3)
    radial_line = padded[:, :, 3:-3, 3:-3]
    axial_line = padded[:, 3:-3, :, 3:-3]
    azimuth_line = padded[:, 3:-3, 3:-3, :]
    lower_rim = jnp.where(row_id == 0, mirror, radial_line[:, :3])
    upper_rim = jnp.where(row_id == row_count - 1, outer_rim, radial_line[:, -3:])
    radial_line = jnp.concatenate([lower_rim, fields, upper_rim], 1)
    tendencies = tendency(fields, radial_line, axial_line, azimuth_line, row_id * cycle_count)
    advanced = 0.75 * state_start + 0.25 * (state_section + time_step * tendencies)
    weights = cycle_weights(cutoff, KMODES, NT)
    filtered = apply_filter(advanced, weights, theta_id)
    inner_next = jnp.where(row_id == 0, filtered, advanced)
    return jnp.concatenate([inner_next, advanced[:, filtered_count:]], 1)


def solution(mesh):
    in_specs = (
        P(None, "row", "gz", "theta"),
        P(None, "row", "gz", "theta"),
        P("row", "gz", "theta"),
        P(),
    )
    out_specs = P(None, "row", "gz", "theta")
    return jax.shard_map(shards, mesh=mesh, in_specs=in_specs, out_specs=out_specs, check_vma=False)
```

profile of v0, /device:TPU:0, one launch (start us, length us, event | category | flops | bytes accessed | tf_op | source)
XLA Modules:
  0.0 148.2 jit_solution(16903499594754744437)
XLA Ops:
  6.6 1.4 bitcast_dynamic-update-slice_fusion
  8.0 1.2 fusion.11
  9.2 3.0 %collective-permute-start.2 = (f32[7,3,32,256]{3,2,1,0:T(8,128)}, f32[7,3,32,256]{3,2,1,0:T(8,128)S(1)}, u32[]{:S(2)}, u32[]{:S(2)}) collective-permute-start(f32[7,3,32,256]{3,2,1,0:T(8,128)} %get-tuple-element.24), channel_id=1, source_target_pairs={{16,0},{0,16},{17,1},{1,17},{18,2},{2,18},{19,3},{3,19},{20,4},{4,... | collective-permute-start | bytes 2064392 | tf_op jit(solution)/shard_map/ppermute | solution.py:32
  12.2 1.5 %collective-permute-start = (f32[7,3,32,256]{3,2,1,0:T(8,128)}, f32[7,3,32,256]{3,2,1,0:T(8,128)}, u32[]{:S(2)}, u32[]{:S(2)}) collective-permute-start(f32[7,3,32,256]{3,2,1,0:T(8,128)} %get-tuple-element.24), channel_id=1, source_target_pairs={{0,8},{4,12},{8,0},{12,4},{1,9},{5,13},{9,1},{13,5},{2,10},{6,14},... | collective-permute-start | bytes 2064392 | tf_op jit(solution)/shard_map/ppermute | solution.py:20
  13.7 0.5 collective-permute-start.1
  14.5 0.6 fusion.47
  15.1 13.7 %collective-permute-done.2 = f32[7,3,32,256]{3,2,1,0:T(8,128)S(1)} collective-permute-done((f32[7,3,32,256]{3,2,1,0:T(8,128)}, f32[7,3,32,256]{3,2,1,0:T(8,128)S(1)}, u32[]{:S(2)}, u32[]{:S(2)}) %collective-permute-start.2) | collective-permute-done | bytes 688160 | tf_op jit(solution)/shard_map/ppermute | solution.py:32
  28.8 13.8 %collective-permute-done.1 = f32[7,3,32,256]{3,2,1,0:T(8,128)S(1)} collective-permute-done((f32[7,3,32,256]{3,2,1,0:T(8,128)}, f32[7,3,32,256]{3,2,1,0:T(8,128)S(1)}, u32[]{:S(2)}, u32[]{:S(2)}) %collective-permute-start.1) | collective-permute-done | bytes 688160 | tf_op jit(solution)/shard_map/ppermute | solution.py:30
  42.6 1.5 %multiply_select_fusion = f32[7,3,32,256]{3,2,1,0:T(8,128)S(1)} fusion(f32[7,3,32,256]{3,2,1,0:T(8,128)S(1)} %collective-permute-done.1, f32[7,3,32,256]{3,2,1,0:T(8,128)} %collective-permute-done, f32[7]{0:T(128)S(1)} %copy-done.10, pred[]{:T(512)S(6)} %eq.25), kind=kLoop, calls=%fused_computation.37 | loop fusion | flops 344064 | bytes 2064413 | tf_op jit(solution)/shard_map/jit(_where)/select_n | solution.py:179
  44.2 1.9 %pad_maximum_fusion.2 = (f32[7,10,32,256]{3,2,1,0:T(8,128)}, f32[7,10,32,256]{3,2,1,0:T(8,128)S(1)}) fusion(f32[7,3,32,256]{3,2,1,0:T(8,128)S(1)} %broadcast_select_fusion, f32[1,4,32,256]{3,2,1,0:T(8,128)S(1)} %bitcast.49, f32[6,4,32,256]{3,2,1,0:T(8,128)S(1)} %copy-done, f32[7,3,32,256]{3,2,1,0:T(8,128)S(1)} %multiply_select_fusion, ...), kind=kLoop, calls=%fused_computation.2 | loop fusion | flops 2867200 | bytes 8257536 | tf_op jit(solution)/shard_map/concatenate | solution.py:181
  46.1 1.8 %fusion.56 = (f32[7,10,32,3]{3,2,1,0:T(8,128)}, f32[7,10,32,3]{3,2,1,0:T(8,128)}) fusion(f32[7,10,32,256]{3,2,1,0:T(8,128)S(1)} %get-tuple-element.22), kind=kLoop, calls=%fused_computation.127 | loop fusion | bytes 107520 | tf_op jit(solution)/shard_map/slice | solution.py:27
  47.9 2.6 %copy.7 = f32[7,10,32,3]{2,0,3,1:T(8,128)} copy(f32[7,10,32,3]{3,2,1,0:T(8,128)} %get-tuple-element.20) | data formatting | bytes 53760 | tf_op jit(solution)/shard_map/slice | solution.py:26
  50.8 2.4 %copy.6 = f32[7,10,32,3]{2,0,3,1:T(8,128)} copy(f32[7,10,32,3]{3,2,1,0:T(8,128)} %get-tuple-element.19) | data formatting | bytes 53760 | tf_op jit(solution)/shard_map/slice | solution.py:27
  53.8 0.7 add_multiply_fusion
  54.5 5.2 %add_multiply_fusion.3 = f32[6,5,32,256]{3,2,1,0:T(8,128)} fusion(f32[6,10,32,256]{3,2,1,0:T(8,128)S(1)} %get-tuple-element.16, f32[6,10,32,256]{3,2,1,0:T(8,128)S(1)} %get-tuple-element.15, f32[5]{0:T(128)S(1)} %add_convert_fusion), kind=kLoop, calls=%fused_computation.20 | loop fusion | flops 31948800 | bytes 10813460 | tf_op jit(solution)/shard_map/mul | solution.py:114
  59.7 1.4 copy.9
  61.1 1.4 copy.8
  62.5 2.6 %pad_maximum_fusion.1 = f32[7,10,32,262]{3,2,1,0:T(8,128)S(1)} fusion(f32[7,10,32,3]{3,2,1,0:T(8,128)S(1)} %copy.9, f32[7,3,32,256]{3,2,1,0:T(8,128)} %copy-done.3, f32[1,4,32,256]{3,2,1,0:T(8,128)S(1)} %bitcast.50, f32[6,4,32,256]{3,2,1,0:T(8,128)S(1)} %copy-done, f32[7,3,32,256]{3,2,1,0:T(8,128)} %copy-done.1, f32[7,10,32,3]{3,2,1,0:T(8,128)S(1)} %copy.8), kind=kLoop, calls=%fused_computation.1 | loop fusion | flops 2934400 | bytes 4695040 | tf_op jit(solution)/shard_map/concatenate | solution.py:28
  65.2 0.9 copy-done.2
  67.4 0.3 fusion.22
  68.0 0.3 add_multiply_fusion.1
  68.3 3.9 %collective-permute-start.6 = (f32[7,10,3,262]{3,2,1,0:T(4,128)S(1)}, f32[7,10,3,262]{3,2,1,0:T(4,128)S(1)}, u32[]{:S(2)}, u32[]{:S(2)}) collective-permute-start(f32[7,10,3,262]{3,2,1,0:T(4,128)S(1)} %get-tuple-element.18), channel_id=1, source_target_pairs={{1,0},{2,1},{3,2},{0,3},{5,4},{6,5},{7,6},{4,7},{9,8},{10,9},{11,1... | collective-permute-start | bytes 660248 | tf_op jit(solution)/shard_map/ppermute | solution.py:32
  72.2 5.9 %divide_add_fusion = f32[6,4,32,257]{3,2,1,0:T(8,128)S(1)} fusion(f32[6,4,32,262]{3,2,1,0:T(8,128)S(1)} %get-tuple-element.14, f32[6,4,32,262]{3,2,1,0:T(8,128)S(1)} %get-tuple-element.13), kind=kLoop, calls=%fused_computation.13 | loop fusion | flops 25461504 | bytes 8684544 | tf_op jit(solution)/shard_map/add | solution.py:103
  78.1 4.3 %collective-permute-done.6 = f32[7,10,3,262]{3,2,1,0:T(4,128)S(1)} collective-permute-done((f32[7,10,3,262]{3,2,1,0:T(4,128)S(1)}, f32[7,10,3,262]{3,2,1,0:T(4,128)S(1)}, u32[]{:S(2)}, u32[]{:S(2)}) %collective-permute-start.6) | collective-permute-done | bytes 220112 | tf_op jit(solution)/shard_map/ppermute | solution.py:32
  82.4 10.1 %collective-permute-done.5 = f32[7,10,3,262]{3,2,1,0:T(4,128)S(1)} collective-permute-done((f32[7,10,3,262]{3,2,1,0:T(4,128)S(1)}, f32[7,10,3,262]{3,2,1,0:T(4,128)S(1)}, u32[]{:S(2)}, u32[]{:S(2)}) %collective-permute-start.5) | collective-permute-done | bytes 220112 | tf_op jit(solution)/shard_map/ppermute | solution.py:30
  92.5 5.7 %pad_maximum_fusion = f32[7,10,38,262]{3,2,1,0:T(8,128)S(1)} fusion(f32[7,10,3,262]{3,2,1,0:T(4,128)S(1)} %collective-permute-done.6, f32[7,10,32,3]{3,2,1,0:T(8,128)S(1)} %copy.9, f32[7,3,32,256]{3,2,1,0:T(8,128)S(1)} %copy-done.4, f32[1,4,32,256]{3,2,1,0:T(8,128)S(1)} %bitcast.57, f32[6,4,32,256]{3,2,1,0:T(8,128)S(1)} %copy-done, ...), kind=kLoop, calls=%fused_computation | loop fusion | flops 4878440 | bytes 5575360 | tf_op jit(solution)/shard_map/concatenate | solution.py:28
  99.1 0.3 add_multiply_fusion.2
  99.4 5.0 %divide_add_fusion.1 = f32[6,4,33,256]{3,2,1,0:T(8,128)S(1)} fusion(f32[6,4,38,256]{3,2,1,0:T(8,128)S(1)} %get-tuple-element.12, f32[6,4,38,256]{3,2,1,0:T(8,128)S(1)} %get-tuple-element.11), kind=kLoop, calls=%fused_computation.17 | loop fusion | flops 26155008 | bytes 8921088 | tf_op jit(solution)/shard_map/add | solution.py:103
  104.5 0.7 fusion.7
  105.2 1.6 %fusion.48 = f32[6,4,32,128]{3,2,1,0:T(8,128)} fusion(f32[6,4,32,256]{3,2,1,0:T(8,128)S(1)} %fusion.7, f32[256,64]{1,0:T(8,128)S(1)} %get-tuple-element.26, f32[256,64]{1,0:T(8,128)S(1)} %get-tuple-element.25), kind=kOutput, calls=%fused_computation.112 | convolution fusion | flops 302022656 | bytes 1310720 | tf_op jit(solution)/shard_map/vizt,tk->vizk/dot_general | solution.py:155
  107.0 31.6 %all-reduce.2.cloned.1.call-done = f32[6,4,32,128]{3,2,1,0:T(8,128)} async-done(((f32[6,4,32,128]{3,2,1,0:T(8,128)}), f32[6,4,32,128]{3,2,1,0:T(8,128)}) %all-reduce.2.cloned.1.call-update) | async-done | bytes 393232 | tf_op jit(solution)/shard_map/psum | solution.py:158
  138.6 2.7 %convolution_select_fusion = f32[6,4,32,256]{3,2,1,0:T(8,128)} fusion(f32[6,4,32,256]{3,2,1,0:T(8,128)S(1)} %fusion.7, f32[6,4,32,128]{3,2,1,0:T(8,128)} %all-reduce.2.cloned.1.call-done, pred[]{:T(512)S(6)} %eq.25, f32[4,128]{1,0:T(4,128)S(1)} %pad_maximum_fusion.8, f32[256,64]{1,0:T(8,128)S(1)} %get-tuple-element.26, f32[256,64]{1,0:T(8,128)S(1)} %get-tuple-element.25), kind=kOutput, calls=%fused_computation.9 | convolution fusion | flops 302317568 | bytes 2099201 | tf_op jit(solution)/shard_map/vizk,tk->vizt/dot_general | solution.py:160
  (62 shorter events, 3.8 us)
Async XLA Ops:
  6.5 1.5 copy-start
  6.5 132.1 %all-reduce.2.cloned.1.call-start = ((), (), s32[]{:S(2)}) async-start(), calls=%async_computation | async-start | bytes 786432 | tf_op jit(solution)/shard_map/psum | solution.py:158
  9.2 19.5 %collective-permute-start.2 = (f32[7,3,32,256]{3,2,1,0:T(8,128)}, f32[7,3,32,256]{3,2,1,0:T(8,128)S(1)}, u32[]{:S(2)}, u32[]{:S(2)}) collective-permute-start(f32[7,3,32,256]{3,2,1,0:T(8,128)} %get-tuple-element.24), channel_id=1, source_target_pairs={{16,0},{0,16},{17,1},{1,17},{18,2},{2,18},{19,3},{3,19},{20,4},{4,... | collective-permute-start | bytes 2064392 | tf_op jit(solution)/shard_map/ppermute | solution.py:32
  12.2 30.4 %collective-permute-start = (f32[7,3,32,256]{3,2,1,0:T(8,128)}, f32[7,3,32,256]{3,2,1,0:T(8,128)}, u32[]{:S(2)}, u32[]{:S(2)}) collective-permute-start(f32[7,3,32,256]{3,2,1,0:T(8,128)} %get-tuple-element.24), channel_id=1, source_target_pairs={{0,8},{4,12},{8,0},{12,4},{1,9},{5,13},{9,1},{13,5},{2,10},{6,14},... | collective-permute-start | bytes 2064392 | tf_op jit(solution)/shard_map/ppermute | solution.py:20
  13.7 28.9 %collective-permute-start.1 = (f32[7,3,32,256]{3,2,1,0:T(8,128)}, f32[7,3,32,256]{3,2,1,0:T(8,128)S(1)}, u32[]{:S(2)}, u32[]{:S(2)}) collective-permute-start(f32[7,3,32,256]{3,2,1,0:T(8,128)} %get-tuple-element.23), channel_id=1, source_target_pairs={{0,16},{16,0},{1,17},{17,1},{2,18},{18,2},{3,19},{19,3},{4,20},{20... | collective-permute-start | bytes 2064392 | tf_op jit(solution)/shard_map/ppermute | solution.py:30
  14.4 28.2 %copy-start.10 = (f32[7]{0:T(128)S(1)}, f32[7]{0:T(128)}, u32[]{:S(2)}) copy-start(f32[7]{0:T(128)} %constant.69.clone) | copy-start | bytes 88
  14.4 29.7 %copy-start.7 = (f32[6,4,32,256]{3,2,1,0:T(8,128)}, f32[6,4,32,256]{3,2,1,0:T(8,128)S(1)}, u32[]{:S(2)}) copy-start(f32[6,4,32,256]{3,2,1,0:T(8,128)S(1)} %broadcast_dynamic-update-slice_fusion) | copy-start | bytes 2359300
  28.7 15.4 %copy-start.3 = (f32[7,3,32,256]{3,2,1,0:T(8,128)}, f32[7,3,32,256]{3,2,1,0:T(8,128)S(1)}, u32[]{:S(2)}) copy-start(f32[7,3,32,256]{3,2,1,0:T(8,128)S(1)} %collective-permute-done.2) | copy-start | bytes 2064388
  42.6 3.5 %copy-start.1 = (f32[7,3,32,256]{3,2,1,0:T(8,128)}, f32[7,3,32,256]{3,2,1,0:T(8,128)S(1)}, u32[]{:S(2)}) copy-start(f32[7,3,32,256]{3,2,1,0:T(8,128)S(1)} %collective-permute-done.1) | copy-start | bytes 2064388
  47.9 5.6 %copy-start.5 = (f32[7,10,32,256]{3,2,1,0:T(8,128)S(1)}, f32[7,10,32,256]{3,2,1,0:T(8,128)}, u32[]{:S(2)}) copy-start(f32[7,10,32,256]{3,2,1,0:T(8,128)} %get-tuple-element.21) | copy-start | bytes 6881284
  50.5 9.2 %collective-permute-start.4 = (f32[7,10,32,3]{2,0,3,1:T(8,128)}, f32[7,10,32,3]{2,0,3,1:T(8,128)}, u32[]{:S(2)}, u32[]{:S(2)}) collective-permute-start(f32[7,10,32,3]{2,0,3,1:T(8,128)} %copy.7), channel_id=1, source_target_pairs={{4,0},{8,4},{12,8},{0,12},{5,1},{9,5},{13,9},{1,13},{6,2},{10,6},{... | collective-permute-start | bytes 80648 | tf_op jit(solution)/shard_map/ppermute | solution.py:32
  53.2 7.9 %collective-permute-start.3 = (f32[7,10,32,3]{2,0,3,1:T(8,128)}, f32[7,10,32,3]{2,0,3,1:T(8,128)}, u32[]{:S(2)}, u32[]{:S(2)}) collective-permute-start(f32[7,10,32,3]{2,0,3,1:T(8,128)} %copy.6), channel_id=1, source_target_pairs={{0,4},{4,8},{8,12},{12,0},{1,5},{5,9},{9,13},{13,1},{2,6},{6,10},{... | collective-permute-start | bytes 80648 | tf_op jit(solution)/shard_map/ppermute | solution.py:30
  65.0 1.1 copy-start.2
  65.1 1.3 copy-start.4
  68.3 14.1 %collective-permute-start.6 = (f32[7,10,3,262]{3,2,1,0:T(4,128)S(1)}, f32[7,10,3,262]{3,2,1,0:T(4,128)S(1)}, u32[]{:S(2)}, u32[]{:S(2)}) collective-permute-start(f32[7,10,3,262]{3,2,1,0:T(4,128)S(1)} %get-tuple-element.18), channel_id=1, source_target_pairs={{1,0},{2,1},{3,2},{0,3},{5,4},{6,5},{7,6},{4,7},{9,8},{10,9},{11,1... | collective-permute-start | bytes 660248 | tf_op jit(solution)/shard_map/ppermute | solution.py:32
  72.2 20.3 %collective-permute-start.5 = (f32[7,10,3,262]{3,2,1,0:T(4,128)S(1)}, f32[7,10,3,262]{3,2,1,0:T(4,128)S(1)}, u32[]{:S(2)}, u32[]{:S(2)}) collective-permute-start(f32[7,10,3,262]{3,2,1,0:T(4,128)S(1)} %get-tuple-element.17), channel_id=1, source_target_pairs={{0,1},{1,2},{2,3},{3,0},{4,5},{5,6},{6,7},{7,4},{8,9},{9,10},{10,1... | collective-permute-start | bytes 660248 | tf_op jit(solution)/shard_map/ppermute | solution.py:30
  99.4 5.0 %copy-start.6 = (f32[6,5,32,256]{3,2,1,0:T(8,128)S(1)}, f32[6,5,32,256]{3,2,1,0:T(8,128)}, u32[]{:S(2)}) copy-start(f32[6,5,32,256]{3,2,1,0:T(8,128)} %add_multiply_fusion.3) | copy-start | bytes 2949124
  99.4 5.0 %copy-start.8 = (f32[6,4,32,256]{3,2,1,0:T(8,128)S(1)}, f32[6,4,32,256]{3,2,1,0:T(8,128)}, u32[]{:S(2)}) copy-start(f32[6,4,32,256]{3,2,1,0:T(8,128)} %copy-done.7) | copy-start | bytes 2359300
  99.4 5.0 %copy-start.9 = (f32[6,4,32,256]{3,2,1,0:T(8,128)S(1)}, f32[6,4,32,256]{3,2,1,0:T(8,128)}, u32[]{:S(2)}) copy-start(f32[6,4,32,256]{3,2,1,0:T(8,128)} %param.5) | copy-start | bytes 2359300
  105.2 1.6 %copy-start.11 = (s32[4]{0:T(128)S(1)}, s32[4]{0:T(128)}, u32[]{:S(2)}) copy-start(s32[4]{0:T(128)} %param.8) | copy-start | bytes 52
Sparse Core Ops, SparseCore 0:
  106.9 31.6 all-reduce.1
where the time goes:
time: 149 us; the launch traced here: 148 us
  waiting for transfers between devices  73.5 us (49%)
  other arithmetic  36.1 us (24%)
  between operations  13.8 us (9%)
  local copies, waits for them, and re-layouts  11 us (7%)
  starting transfers between devices  9.39 us (6%)
  matrix products  4.34 us (3%)
    psum x1, waiting for transfers between devices, apply_filter(): coefficients = lax.psum(coefficients, 'theta')  31.6 us
    ppermute x3, waiting for transfers between devices, with_halo(): lax.ppermute(tail, axis, [(i, (i + 1) % count) for i in range(count)])  23.9 us
    ppermute x3, waiting for transfers between devices, with_halo(): lax.ppermute(head, axis, [((i + 1) % count, i) for i in range(count)])  18 us
    add x2, other arithmetic, face_fluxes(): return upwind_part + downwind_part  10.9 us
    concatenate x2, other arithmetic, with_halo(): jnp.concatenate([lax.ppermute(tail, axis, [(i, (i + 1) % count) for i in...  8.27 us
    ppermute x3, starting transfers between devices, with_halo(): lax.ppermute(head, axis, [((i + 1) % count, i) for i in range(count)])  7.17 us
    mul x1, other arithmetic, tendency(): weighted = face_radius * radial_flux  5.18 us
    slice x3, local copies, waits for them, and re-layouts, with_halo(): lax.slice_in_dim(cells, cells.shape[dim] - width, cells.shape[dim], axis=...  4.38 us
  transfers between devices with their start and end apart: 8, of which 5 were waited for; matrix products, arithmetic and copies ran while one was open for 11% of the time, Pallas kernels for 0%

commit v1 on v0

--- a/solution.py
+++ b/solution.py
@@ -155,7 +155,7 @@
     coefficients = jnp.einsum(
         "vizt,tk->vizk", cycle_block, fourier_table, precision=lax.Precision.HIGHEST
     )
-    coefficients = lax.psum(coefficients, "theta")
+    coefficients = jnp.sum(lax.all_gather(coefficients, "theta"), axis=0)
     coefficients = coefficients * weights[None, :, None, :]
     return jnp.einsum("vizk,tk->vizt", coefficients, fourier_table, precision=lax.Precision.HIGHEST)
 

time: 149 us -> 136 us (0.913)
  waiting for transfers between devices: 73.5 us -> 60.4 us
  other arithmetic: 36.1 us -> 37.7 us
    psum x1 -> x0, waiting for transfers between devices: 31.6 us -> none  [apply_filter(): coefficients = lax.psum(coefficients, 'theta')]
    all_gather x0 -> x1, waiting for transfers between devices: none -> 18.5 us  [apply_filter(): coefficients = jnp.sum(lax.all_gather(coefficients, 'theta'), axis=0)]
    reduce_sum x0 -> x1, other arithmetic: none -> 1.6 us  [apply_filter(): coefficients = jnp.sum(lax.all_gather(coefficients, 'theta'), axis=0)]
  transfers between devices with their start and end apart: 8 -> 8, of which waited for: 5 -> 5; matrix products, arithmetic and copies ran while one was open for 11% -> 12% of each run, Pallas kernels for 0% -> 0%
where the time goes in v1:
time: 136 us
  waiting for transfers between devices  60.4 us (44%)
  other arithmetic  37.7 us (28%)
  between operations  13.8 us (10%)
  local copies, waits for them, and re-layouts  11 us (8%)
  starting transfers between devices  9.39 us (7%)
  matrix products  3.35 us (2%)
    ppermute x3, waiting for transfers between devices, with_halo(): lax.ppermute(tail, axis, [(i, (i + 1) % count) for i in range(count)])  23.9 us
    all_gather x1, waiting for transfers between devices, apply_filter(): coefficients = jnp.sum(lax.all_gather(coefficients, 'theta'), axis=0)  18.5 us
    ppermute x3, waiting for transfers between devices, with_halo(): lax.ppermute(head, axis, [((i + 1) % count, i) for i in range(count)])  18 us
    add x2, other arithmetic, face_fluxes(): return upwind_part + downwind_part  10.9 us
    concatenate x2, other arithmetic, with_halo(): jnp.concatenate([lax.ppermute(tail, axis, [(i, (i + 1) % count) for i in...  8.27 us
    ppermute x3, starting transfers between devices, with_halo(): lax.ppermute(head, axis, [((i + 1) % count, i) for i in range(count)])  7.17 us
    mul x1, other arithmetic, tendency(): weighted = face_radius * radial_flux  5.18 us
    slice x3, local copies, waits for them, and re-layouts, with_halo(): lax.slice_in_dim(cells, cells.shape[dim] - width, cells.shape[dim], axis=...  4.38 us
  transfers between devices with their start and end apart: 8, of which 5 were waited for; matrix products, arithmetic and copies ran while one was open for 12% of the time, Pallas kernels for 0%

profile of v1, /device:TPU:0, one launch (start us, length us, event | category | flops | bytes accessed | tf_op | source)
XLA Modules:
  0.0 135.7 jit_solution(9670159649851151030)
XLA Ops:
  6.6 1.4 %bitcast_dynamic-update-slice_fusion = (f32[6,4,32,256]{3,2,1,0:T(8,128)S(1)}, f32[4,32,256]{2,1,0:T(8,128)S(1)}) fusion(f32[6,4,32,256]{3,2,1,0:T(8,128)S(1)} %broadcast_dynamic-update-slice_fusion.1, f32[6,4,32,256]{3,2,1,0:T(8,128)} %param.6, f32[4]{0:T(128)S(1)} %get-tuple-element.28, s32[4,32,256]{2,1,0:T(8,128)} %param.7), kind=kLoop, calls=%fused_computation.96 | loop fusion | flops 622592 | bytes 1049088
  8.0 1.2 fusion.11
  9.2 3.0 %collective-permute-start.2 = (f32[7,3,32,256]{3,2,1,0:T(8,128)}, f32[7,3,32,256]{3,2,1,0:T(8,128)S(1)}, u32[]{:S(2)}, u32[]{:S(2)}) collective-permute-start(f32[7,3,32,256]{3,2,1,0:T(8,128)} %get-tuple-element.24), channel_id=1, source_target_pairs={{16,0},{0,16},{17,1},{1,17},{18,2},{2,18},{19,3},{3,19},{20,4},{4,... | collective-permute-start | bytes 2064392 | tf_op jit(solution)/shard_map/ppermute | solution.py:32
  12.2 1.5 %collective-permute-start = (f32[7,3,32,256]{3,2,1,0:T(8,128)}, f32[7,3,32,256]{3,2,1,0:T(8,128)}, u32[]{:S(2)}, u32[]{:S(2)}) collective-permute-start(f32[7,3,32,256]{3,2,1,0:T(8,128)} %get-tuple-element.24), channel_id=1, source_target_pairs={{0,8},{4,12},{8,0},{12,4},{1,9},{5,13},{9,1},{13,5},{2,10},{6,14},... | collective-permute-start | bytes 2064392 | tf_op jit(solution)/shard_map/ppermute | solution.py:20
  13.7 0.5 collective-permute-start.1
  14.4 0.6 fusion.47
  15.0 13.7 %collective-permute-done.2 = f32[7,3,32,256]{3,2,1,0:T(8,128)S(1)} collective-permute-done((f32[7,3,32,256]{3,2,1,0:T(8,128)}, f32[7,3,32,256]{3,2,1,0:T(8,128)S(1)}, u32[]{:S(2)}, u32[]{:S(2)}) %collective-permute-start.2) | collective-permute-done | bytes 688160 | tf_op jit(solution)/shard_map/ppermute | solution.py:32
  28.8 13.8 %collective-permute-done.1 = f32[7,3,32,256]{3,2,1,0:T(8,128)S(1)} collective-permute-done((f32[7,3,32,256]{3,2,1,0:T(8,128)}, f32[7,3,32,256]{3,2,1,0:T(8,128)S(1)}, u32[]{:S(2)}, u32[]{:S(2)}) %collective-permute-start.1) | collective-permute-done | bytes 688160 | tf_op jit(solution)/shard_map/ppermute | solution.py:30
  42.6 1.5 %multiply_select_fusion = f32[7,3,32,256]{3,2,1,0:T(8,128)S(1)} fusion(f32[7,3,32,256]{3,2,1,0:T(8,128)S(1)} %collective-permute-done.1, f32[7,3,32,256]{3,2,1,0:T(8,128)} %collective-permute-done, f32[7]{0:T(128)S(1)} %copy-done.10, pred[]{:T(512)S(6)} %eq.25), kind=kLoop, calls=%fused_computation.37 | loop fusion | flops 344064 | bytes 2064413 | tf_op jit(solution)/shard_map/jit(_where)/select_n | solution.py:179
  44.2 1.9 %pad_maximum_fusion.2 = (f32[7,10,32,256]{3,2,1,0:T(8,128)}, f32[7,10,32,256]{3,2,1,0:T(8,128)S(1)}) fusion(f32[7,3,32,256]{3,2,1,0:T(8,128)S(1)} %broadcast_select_fusion, f32[1,4,32,256]{3,2,1,0:T(8,128)S(1)} %bitcast.50, f32[6,4,32,256]{3,2,1,0:T(8,128)S(1)} %copy-done, f32[7,3,32,256]{3,2,1,0:T(8,128)S(1)} %multiply_select_fusion, ...), kind=kLoop, calls=%fused_computation.2 | loop fusion | flops 2867200 | bytes 8257536 | tf_op jit(solution)/shard_map/concatenate | solution.py:181
  46.1 1.8 %fusion.56 = (f32[7,10,32,3]{3,2,1,0:T(8,128)}, f32[7,10,32,3]{3,2,1,0:T(8,128)}) fusion(f32[7,10,32,256]{3,2,1,0:T(8,128)S(1)} %get-tuple-element.22), kind=kLoop, calls=%fused_computation.127 | loop fusion | bytes 107520 | tf_op jit(solution)/shard_map/slice | solution.py:27
  47.9 2.6 %copy.7 = f32[7,10,32,3]{2,0,3,1:T(8,128)} copy(f32[7,10,32,3]{3,2,1,0:T(8,128)} %get-tuple-element.20) | data formatting | bytes 53760 | tf_op jit(solution)/shard_map/slice | solution.py:26
  50.8 2.4 %copy.6 = f32[7,10,32,3]{2,0,3,1:T(8,128)} copy(f32[7,10,32,3]{3,2,1,0:T(8,128)} %get-tuple-element.19) | data formatting | bytes 53760 | tf_op jit(solution)/shard_map/slice | solution.py:27
  53.8 0.7 add_multiply_fusion
  54.5 5.2 %add_multiply_fusion.3 = f32[6,5,32,256]{3,2,1,0:T(8,128)} fusion(f32[6,10,32,256]{3,2,1,0:T(8,128)S(1)} %get-tuple-element.16, f32[6,10,32,256]{3,2,1,0:T(8,128)S(1)} %get-tuple-element.15, f32[5]{0:T(128)S(1)} %add_convert_fusion), kind=kLoop, calls=%fused_computation.20 | loop fusion | flops 31948800 | bytes 10813460 | tf_op jit(solution)/shard_map/mul | solution.py:114
  59.7 1.4 %copy.9 = f32[7,10,32,3]{3,2,1,0:T(8,128)S(1)} copy(f32[7,10,32,3]{2,0,3,1:T(8,128)} %collective-permute-done.4) | data formatting | bytes 53760 | tf_op jit(solution)/shard_map/ppermute | solution.py:32
  61.1 1.4 %copy.8 = f32[7,10,32,3]{3,2,1,0:T(8,128)S(1)} copy(f32[7,10,32,3]{2,0,3,1:T(8,128)} %collective-permute-done.3) | data formatting | bytes 53760 | tf_op jit(solution)/shard_map/ppermute | solution.py:30
  62.5 2.6 %pad_maximum_fusion.1 = f32[7,10,32,262]{3,2,1,0:T(8,128)S(1)} fusion(f32[7,10,32,3]{3,2,1,0:T(8,128)S(1)} %copy.9, f32[7,3,32,256]{3,2,1,0:T(8,128)} %copy-done.3, f32[1,4,32,256]{3,2,1,0:T(8,128)S(1)} %bitcast.51, f32[6,4,32,256]{3,2,1,0:T(8,128)S(1)} %copy-done, f32[7,3,32,256]{3,2,1,0:T(8,128)} %copy-done.1, f32[7,10,32,3]{3,2,1,0:T(8,128)S(1)} %copy.8), kind=kLoop, calls=%fused_computation.1 | loop fusion | flops 2934400 | bytes 4695040 | tf_op jit(solution)/shard_map/concatenate | solution.py:28
  65.2 0.9 copy-done.2
  67.4 0.3 fusion.22
  68.0 0.3 add_multiply_fusion.1
  68.4 3.9 %collective-permute-start.6 = (f32[7,10,3,262]{3,2,1,0:T(4,128)S(1)}, f32[7,10,3,262]{3,2,1,0:T(4,128)S(1)}, u32[]{:S(2)}, u32[]{:S(2)}) collective-permute-start(f32[7,10,3,262]{3,2,1,0:T(4,128)S(1)} %get-tuple-element.18), channel_id=1, source_target_pairs={{1,0},{2,1},{3,2},{0,3},{5,4},{6,5},{7,6},{4,7},{9,8},{10,9},{11,1... | collective-permute-start | bytes 660248 | tf_op jit(solution)/shard_map/ppermute | solution.py:32
  72.2 5.9 %divide_add_fusion = f32[6,4,32,257]{3,2,1,0:T(8,128)S(1)} fusion(f32[6,4,32,262]{3,2,1,0:T(8,128)S(1)} %get-tuple-element.14, f32[6,4,32,262]{3,2,1,0:T(8,128)S(1)} %get-tuple-element.13), kind=kLoop, calls=%fused_computation.13 | loop fusion | flops 25461504 | bytes 8684544 | tf_op jit(solution)/shard_map/add | solution.py:103
  78.1 4.3 %collective-permute-done.6 = f32[7,10,3,262]{3,2,1,0:T(4,128)S(1)} collective-permute-done((f32[7,10,3,262]{3,2,1,0:T(4,128)S(1)}, f32[7,10,3,262]{3,2,1,0:T(4,128)S(1)}, u32[]{:S(2)}, u32[]{:S(2)}) %collective-permute-start.6) | collective-permute-done | bytes 220112 | tf_op jit(solution)/shard_map/ppermute | solution.py:32
  82.4 10.1 %collective-permute-done.5 = f32[7,10,3,262]{3,2,1,0:T(4,128)S(1)} collective-permute-done((f32[7,10,3,262]{3,2,1,0:T(4,128)S(1)}, f32[7,10,3,262]{3,2,1,0:T(4,128)S(1)}, u32[]{:S(2)}, u32[]{:S(2)}) %collective-permute-start.5) | collective-permute-done | bytes 220112 | tf_op jit(solution)/shard_map/ppermute | solution.py:30
  92.5 5.7 %pad_maximum_fusion = f32[7,10,38,262]{3,2,1,0:T(8,128)S(1)} fusion(f32[7,10,3,262]{3,2,1,0:T(4,128)S(1)} %collective-permute-done.6, f32[7,10,32,3]{3,2,1,0:T(8,128)S(1)} %copy.9, f32[7,3,32,256]{3,2,1,0:T(8,128)S(1)} %copy-done.4, f32[1,4,32,256]{3,2,1,0:T(8,128)S(1)} %bitcast.58, f32[6,4,32,256]{3,2,1,0:T(8,128)S(1)} %copy-done, ...), kind=kLoop, calls=%fused_computation | loop fusion | flops 4878440 | bytes 5575360 | tf_op jit(solution)/shard_map/concatenate | solution.py:28
  99.4 5.0 %divide_add_fusion.1 = f32[6,4,33,256]{3,2,1,0:T(8,128)S(1)} fusion(f32[6,4,38,256]{3,2,1,0:T(8,128)S(1)} %get-tuple-element.12, f32[6,4,38,256]{3,2,1,0:T(8,128)S(1)} %get-tuple-element.11), kind=kLoop, calls=%fused_computation.17 | loop fusion | flops 26155008 | bytes 8921088 | tf_op jit(solution)/shard_map/add | solution.py:103
  104.5 0.7 fusion.7
  105.2 1.6 %fusion.48 = f32[6,4,32,128]{3,2,1,0:T(8,128)} fusion(f32[6,4,32,256]{3,2,1,0:T(8,128)S(1)} %fusion.7, f32[256,64]{1,0:T(8,128)S(1)} %get-tuple-element.26, f32[256,64]{1,0:T(8,128)S(1)} %get-tuple-element.25), kind=kOutput, calls=%fused_computation.112 | convolution fusion | flops 302022656 | bytes 1310720 | tf_op jit(solution)/shard_map/vizt,tk->vizk/dot_general | solution.py:155
  107.0 18.5 %all-gather.3.cloned.1.call-done = f32[24,4,32,128]{3,2,1,0:T(8,128)} async-done(((f32[6,4,32,128]{3,2,1,0:T(8,128)}), f32[24,4,32,128]{3,2,1,0:T(8,128)}) %all-gather.3.cloned.1.call-update) | async-done | bytes 1572880 | tf_op jit(solution)/shard_map/all_gather | solution.py:158
  125.5 1.6 %reduce_sum.9 = f32[6,4,32,128]{3,2,1,0:T(8,128)S(1)} reduce(f32[4,6,4,32,128]{4,3,2,1,0:T(8,128)} %bitcast.59, f32[]{:T(128)} %constant.39.clone.1), dimensions={0}, to_apply=%region_0.1 | reduce | flops 294912 | bytes 1966084 | tf_op jit(solution)/shard_map/reduce_sum | solution.py:158
  127.1 1.7 %convolution_select_fusion = f32[6,4,32,256]{3,2,1,0:T(8,128)} fusion(f32[6,4,32,256]{3,2,1,0:T(8,128)S(1)} %fusion.7, f32[6,4,32,128]{3,2,1,0:T(8,128)S(1)} %reduce_sum.9, pred[]{:T(512)S(6)} %eq.25, f32[4,128]{1,0:T(4,128)S(1)} %pad_maximum_fusion.8, f32[256,64]{1,0:T(8,128)S(1)} %get-tuple-element.26, f32[256,64]{1,0:T(8,128)S(1)} %get-tuple-element.25), kind=kOutput, calls=%fused_computation.9 | convolution fusion | flops 302317568 | bytes 2099201 | tf_op jit(solution)/shard_map/vizk,tk->vizt/dot_general | solution.py:160
  (63 shorter events, 4.1 us)
Async XLA Ops:
  6.5 1.5 %copy-start = (f32[6,4,32,256]{3,2,1,0:T(8,128)S(1)}, f32[6,4,32,256]{3,2,1,0:T(8,128)}, u32[]{:S(2)}) copy-start(f32[6,4,32,256]{3,2,1,0:T(8,128)} %param.6) | copy-start | bytes 2359300
  6.5 118.9 %all-gather.3.cloned.1.call-start = ((), (), s32[]{:S(2)}) async-start(), calls=%async_computation | async-start | bytes 1966080 | tf_op jit(solution)/shard_map/all_gather | solution.py:158
  9.2 19.5 %collective-permute-start.2 = (f32[7,3,32,256]{3,2,1,0:T(8,128)}, f32[7,3,32,256]{3,2,1,0:T(8,128)S(1)}, u32[]{:S(2)}, u32[]{:S(2)}) collective-permute-start(f32[7,3,32,256]{3,2,1,0:T(8,128)} %get-tuple-element.24), channel_id=1, source_target_pairs={{16,0},{0,16},{17,1},{1,17},{18,2},{2,18},{19,3},{3,19},{20,4},{4,... | collective-permute-start | bytes 2064392 | tf_op jit(solution)/shard_map/ppermute | solution.py:32
  12.2 30.4 %collective-permute-start = (f32[7,3,32,256]{3,2,1,0:T(8,128)}, f32[7,3,32,256]{3,2,1,0:T(8,128)}, u32[]{:S(2)}, u32[]{:S(2)}) collective-permute-start(f32[7,3,32,256]{3,2,1,0:T(8,128)} %get-tuple-element.24), channel_id=1, source_target_pairs={{0,8},{4,12},{8,0},{12,4},{1,9},{5,13},{9,1},{13,5},{2,10},{6,14},... | collective-permute-start | bytes 2064392 | tf_op jit(solution)/shard_map/ppermute | solution.py:20
  13.7 28.9 %collective-permute-start.1 = (f32[7,3,32,256]{3,2,1,0:T(8,128)}, f32[7,3,32,256]{3,2,1,0:T(8,128)S(1)}, u32[]{:S(2)}, u32[]{:S(2)}) collective-permute-start(f32[7,3,32,256]{3,2,1,0:T(8,128)} %get-tuple-element.23), channel_id=1, source_target_pairs={{0,16},{16,0},{1,17},{17,1},{2,18},{18,2},{3,19},{19,3},{4,20},{20... | collective-permute-start | bytes 2064392 | tf_op jit(solution)/shard_map/ppermute | solution.py:30
  14.4 28.3 %copy-start.10 = (f32[7]{0:T(128)S(1)}, f32[7]{0:T(128)}, u32[]{:S(2)}) copy-start(f32[7]{0:T(128)} %constant.69.clone) | copy-start | bytes 88
  14.4 29.7 %copy-start.7 = (f32[6,4,32,256]{3,2,1,0:T(8,128)}, f32[6,4,32,256]{3,2,1,0:T(8,128)S(1)}, u32[]{:S(2)}) copy-start(f32[6,4,32,256]{3,2,1,0:T(8,128)S(1)} %broadcast_dynamic-update-slice_fusion) | copy-start | bytes 2359300
  28.7 15.4 %copy-start.3 = (f32[7,3,32,256]{3,2,1,0:T(8,128)}, f32[7,3,32,256]{3,2,1,0:T(8,128)S(1)}, u32[]{:S(2)}) copy-start(f32[7,3,32,256]{3,2,1,0:T(8,128)S(1)} %collective-permute-done.2) | copy-start | bytes 2064388
  42.6 3.5 %copy-start.1 = (f32[7,3,32,256]{3,2,1,0:T(8,128)}, f32[7,3,32,256]{3,2,1,0:T(8,128)S(1)}, u32[]{:S(2)}) copy-start(f32[7,3,32,256]{3,2,1,0:T(8,128)S(1)} %collective-permute-done.1) | copy-start | bytes 2064388
  47.9 5.6 %copy-start.5 = (f32[7,10,32,256]{3,2,1,0:T(8,128)S(1)}, f32[7,10,32,256]{3,2,1,0:T(8,128)}, u32[]{:S(2)}) copy-start(f32[7,10,32,256]{3,2,1,0:T(8,128)} %get-tuple-element.21) | copy-start | bytes 6881284
  50.5 9.2 %collective-permute-start.4 = (f32[7,10,32,3]{2,0,3,1:T(8,128)}, f32[7,10,32,3]{2,0,3,1:T(8,128)}, u32[]{:S(2)}, u32[]{:S(2)}) collective-permute-start(f32[7,10,32,3]{2,0,3,1:T(8,128)} %copy.7), channel_id=1, source_target_pairs={{4,0},{8,4},{12,8},{0,12},{5,1},{9,5},{13,9},{1,13},{6,2},{10,6},{... | collective-permute-start | bytes 80648 | tf_op jit(solution)/shard_map/ppermute | solution.py:32
  53.2 7.9 %collective-permute-start.3 = (f32[7,10,32,3]{2,0,3,1:T(8,128)}, f32[7,10,32,3]{2,0,3,1:T(8,128)}, u32[]{:S(2)}, u32[]{:S(2)}) collective-permute-start(f32[7,10,32,3]{2,0,3,1:T(8,128)} %copy.6), channel_id=1, source_target_pairs={{0,4},{4,8},{8,12},{12,0},{1,5},{5,9},{9,13},{13,1},{2,6},{6,10},{... | collective-permute-start | bytes 80648 | tf_op jit(solution)/shard_map/ppermute | solution.py:30
  65.1 1.1 copy-start.2
  65.1 1.3 copy-start.4
  68.4 14.1 %collective-permute-start.6 = (f32[7,10,3,262]{3,2,1,0:T(4,128)S(1)}, f32[7,10,3,262]{3,2,1,0:T(4,128)S(1)}, u32[]{:S(2)}, u32[]{:S(2)}) collective-permute-start(f32[7,10,3,262]{3,2,1,0:T(4,128)S(1)} %get-tuple-element.18), channel_id=1, source_target_pairs={{1,0},{2,1},{3,2},{0,3},{5,4},{6,5},{7,6},{4,7},{9,8},{10,9},{11,1... | collective-permute-start | bytes 660248 | tf_op jit(solution)/shard_map/ppermute | solution.py:32
  72.2 20.3 %collective-permute-start.5 = (f32[7,10,3,262]{3,2,1,0:T(4,128)S(1)}, f32[7,10,3,262]{3,2,1,0:T(4,128)S(1)}, u32[]{:S(2)}, u32[]{:S(2)}) collective-permute-start(f32[7,10,3,262]{3,2,1,0:T(4,128)S(1)} %get-tuple-element.17), channel_id=1, source_target_pairs={{0,1},{1,2},{2,3},{3,0},{4,5},{5,6},{6,7},{7,4},{8,9},{9,10},{10,1... | collective-permute-start | bytes 660248 | tf_op jit(solution)/shard_map/ppermute | solution.py:30
  99.4 5.0 %copy-start.6 = (f32[6,5,32,256]{3,2,1,0:T(8,128)S(1)}, f32[6,5,32,256]{3,2,1,0:T(8,128)}, u32[]{:S(2)}) copy-start(f32[6,5,32,256]{3,2,1,0:T(8,128)} %add_multiply_fusion.3) | copy-start | bytes 2949124
  99.4 5.0 %copy-start.8 = (f32[6,4,32,256]{3,2,1,0:T(8,128)S(1)}, f32[6,4,32,256]{3,2,1,0:T(8,128)}, u32[]{:S(2)}) copy-start(f32[6,4,32,256]{3,2,1,0:T(8,128)} %copy-done.7) | copy-start | bytes 2359300
  99.4 5.0 %copy-start.9 = (f32[6,4,32,256]{3,2,1,0:T(8,128)S(1)}, f32[6,4,32,256]{3,2,1,0:T(8,128)}, u32[]{:S(2)}) copy-start(f32[6,4,32,256]{3,2,1,0:T(8,128)} %param.5) | copy-start | bytes 2359300
  105.2 1.7 %copy-start.11 = (s32[4]{0:T(128)S(1)}, s32[4]{0:T(128)}, u32[]{:S(2)}) copy-start(s32[4]{0:T(128)} %param.8) | copy-start | bytes 52
Sparse Core Ops, SparseCore 0:
  107.0 18.4 all-gather.2
